TPU v7x, 32 devices: a whole 2x2x4 slice. The times are simulated.
32 devices in a mesh: row: 4 (over y, x), col: 8 (over z, core).
Axes of the slice: x: 2, y: 2, z: 4, core: 2. Of those that a mesh axis runs over, the one named last changes fastest.
Arguments:
- covariance: float32 [16384, 16384], P('row', 'col'), may hold values from -1 to 560
- seed_index: int32 [128], replicated, may hold values from 0 to 16383, as said below
Outputs:
- basis: float32 [16384, 384], P('row')
- projection: float32 [384, 256], replicated
- first_pass: float32 [384, 256], replicated
Inputs may be any that keep to these rules, and one draw needn't show every extreme that they name: `seed_index`: 128 distinct column indices.
All inputs are finite; a program needn't handle non-finite values.
Results may differ from a plain program's by a relative error of at most 0.00019.
Values sent between devices are 32-bit elements; how exact they have to be, the bound alone decides.
A program may use at most 128 MiB of HBM per device.

v0:
```python
import jax
import jax.numpy as jnp
from jax import lax
from jax.sharding import PartitionSpec as P

N = 16384
ITERS = 2


def product(left, right):
    return jnp.dot(left, right, precision=lax.Precision.HIGHEST, preferred_element_type=jnp.float32)


def finish_block(block, gram):
    lower = jnp.linalg.cholesky(gram)
    basis_block = jax.scipy.linalg.solve_triangular(lower, block.T, lower=True).T
    return (basis_block, lower.T)


def transpose_block(current, col_place, col_count):
    whole = lax.all_gather(current, "row", axis=0, tiled=True)
    vector = lax.dynamic_slice_in_dim(whole, col_place * col_count, col_count, 0)
    return vector


def local(covariance, seed_index):
    col_count = covariance.shape[1]
    width = seed_index.shape[0]
    col_place = lax.axis_index("col")
    offsets = seed_index - col_place * col_count
    inside = (offsets >= 0) & (offsets < col_count)
    picked = jnp.take(covariance, jnp.clip(offsets, 0, col_count - 1), axis=1)
    start = lax.psum(jnp.where(inside[None, :], picked, 0.0), "col")
    gram = lax.psum(product(start.T, start), "row")
    current, upper = finish_block(start, gram)
    full = current
    blocks = [current]
    projection = jnp.zeros(((ITERS + 1) * width, ITERS * width), jnp.float32)
    first_pass = jnp.zeros(((ITERS + 1) * width, ITERS * width), jnp.float32)
    for section in range(ITERS):
        vector = transpose_block(full, col_place, col_count)
        partial_value = product(covariance, vector)
        stacked = jnp.concatenate(blocks, axis=1)
        image = lax.psum(partial_value, "col")
        first = lax.psum(product(stacked.T, image), "row")
        once = image - product(stacked, first)
        second, raw_gram = lax.psum((product(stacked.T, once), product(once.T, once)), "row")
        twice = once - product(stacked, second)
        gram = raw_gram - product(second.T, second)
        current, upper = finish_block(twice, gram)
        projection = projection.at[
            : (section + 1) * width, section * width : (section + 1) * width
        ].set(first + second)
        projection = projection.at[
            (section + 1) * width : (section + 2) * width, section * width : (section + 1) * width
        ].set(upper)
        first_pass = first_pass.at[
            : (section + 1) * width, section * width : (section + 1) * width
        ].set(first)
        blocks.append(current)
        full = current
    basis = jnp.concatenate(blocks, axis=1) * jnp.float32(N**0.5)
    return (basis, projection, first_pass)


def solution(mesh):
    return jax.shard_map(
        local,
        mesh=mesh,
        in_specs=(P("row", "col"), P()),
        out_specs=(P("row", None), P(), P()),
        check_vma=False,
    )
```

profile of v0, /device:TPU:0, one launch (start us, length us, event | category | flops | bytes accessed | tf_op | source)
XLA Modules:
  0.0 872.2 jit_solution(4701074359064413226)
XLA Ops:
  7.2 0.7 compare_and_fusion
  7.9 31.2 %copy.5 = f32[4096,2048]{0,1:T(8,128)} copy(f32[4096,2048]{1,0:T(8,128)} %param.17) | data formatting | bytes 67108864 | tf_op args[0]
  39.1 12.8 %gather_fusion = f32[128,4096]{1,0:T(8,128)S(1)} fusion(f32[4096,2048]{0,1:T(8,128)} %copy.5, s32[1024]{0:T(1024)S(1)} %pad_clamp_fusion), kind=kCustom, calls=%fused_computation | custom fusion | bytes 4194816 | tf_op jit(solution)/shard_map/jit(_take)/gather | solution.py:32
  51.8 1.7 select_bitcast_fusion
  53.6 68.0 %all-reduce.13.cloned.1.call-done = f32[4096,128]{0,1:T(8,128)} async-done(((f32[4096,128]{0,1:T(8,128)}), f32[4096,128]{0,1:T(8,128)}) %all-reduce.13.cloned.1.call-update) | async-done | bytes 2097168 | tf_op jit(solution)/shard_map/psum | solution.py:33
  121.6 4.8 fusion.25
  126.8 41.3 %all-reduce.15.cloned.1.call-done = f32[128,128]{0,1:T(8,128)} async-done(((f32[128,128]{0,1:T(8,128)}), f32[128,128]{0,1:T(8,128)}) %all-reduce.15.cloned.1.call-update) | async-done | bytes 65552 | tf_op jit(solution)/shard_map/psum | solution.py:34
  168.0 0.9 copy.7
  169.0 0.9 fusion.15
  169.8 11.7 %cholesky.59 = f32[128,128]{1,0:T(8,128)S(1)} custom-call(f32[128,128]{1,0:T(8,128)S(1)} %fusion.15), custom_call_target="Cholesky" | custom-call | tf_op jit(solution)/shard_map/jit(cholesky)/cholesky | solution.py:15
  182.2 0.7 fusion.9
  182.9 9.8 %custom-call.7 = f32[1,128,128]{1,2,0:T(8,128)S(1)} custom-call(f32[1,128,128]{2,1,0:T(8,128)S(1)} %fusion.9), custom_call_target="InvertDiagBlocksLowerTriangular" | custom-call | tf_op jit(solution)/shard_map/jit(_solve_triangular)/triangular_solve | solution.py:16
  192.7 3.2 fusion.2
  196.5 87.1 %all-gather.3.cloned.1.call-done = f32[16384,128]{0,1:T(8,128)} async-done(((f32[4096,128]{0,1:T(8,128)}), f32[16384,128]{0,1:T(8,128)}) %all-gather.3.cloned.1.call-update) | async-done | bytes 8388624 | tf_op jit(solution)/shard_map/all_gather | solution.py:21
  283.6 39.2 %convolution_bitcast_fusion.3 = f32[4096,128]{0,1:T(8,128)} fusion(f32[4096,2048]{1,0:T(8,128)} %param.17, f32[16384,128]{0,1:T(8,128)} %all-gather.3.cloned.1.call-done, s32[]{:T(128)S(6)} %select_n.23), kind=kOutput, calls=%fused_computation.11 | convolution fusion | flops 12884901888 | bytes 36700164 | tf_op jit(solution)/shard_map/dot_general | solution.py:11
  322.9 65.2 %all-reduce.17.cloned.1.call-done = f32[4096,128]{0,1:T(8,128)} async-done(((f32[4096,128]{0,1:T(8,128)}), f32[4096,128]{0,1:T(8,128)}) %all-reduce.17.cloned.1.call-update) | async-done | bytes 2097168 | tf_op jit(solution)/shard_map/psum | solution.py:44
  388.1 4.0 fusion.26
  392.4 41.4 %all-reduce.19.cloned.1.call-done = f32[128,128]{1,0:T(8,128)} async-done(((f32[128,128]{1,0:T(8,128)}), f32[128,128]{1,0:T(8,128)}) %all-reduce.19.cloned.1.call-update) | async-done | bytes 65552 | tf_op jit(solution)/shard_map/psum | solution.py:45
  433.8 3.7 convolution_subtract_fusion.3
  437.5 2.4 fusion.27
  439.9 2.5 fusion.28
  442.7 42.2 %all-reduce.27.cloned.1.call-done = (f32[128,128]{1,0:T(8,128)}, f32[128,128]{0,1:T(8,128)}) async-done(((f32[128,128]{1,0:T(8,128)}, f32[128,128]{0,1:T(8,128)}), (f32[128,128]{1,0:T(8,128)}, f32[128,128]{0,1:T(8,128)})) %all-reduce.27.cloned.1.call-update) | async-done | bytes 131088 | tf_op jit(solution)/shard_map/psum | solution.py:47
  484.9 5.0 fusion.1
  490.3 11.7 %cholesky.70 = f32[128,128]{1,0:T(8,128)S(1)} custom-call(f32[128,128]{1,0:T(8,128)S(1)} %fusion.13), custom_call_target="Cholesky" | custom-call | tf_op jit(solution)/shard_map/jit(cholesky)/cholesky | solution.py:15
  502.7 0.7 fusion.16
  503.3 9.8 %custom-call.8 = f32[1,128,128]{1,2,0:T(8,128)S(1)} custom-call(f32[1,128,128]{2,1,0:T(8,128)S(1)} %get-tuple-element.91), custom_call_target="InvertDiagBlocksLowerTriangular" | custom-call | tf_op jit(solution)/shard_map/jit(_solve_triangular)/triangular_solve | solution.py:16
  513.1 4.9 convolution_bitcast_fusion.2
  518.5 87.2 %all-gather.5.cloned.1.call-done = f32[16384,128]{0,1:T(8,128)} async-done(((f32[4096,128]{0,1:T(8,128)}), f32[16384,128]{0,1:T(8,128)}) %all-gather.5.cloned.1.call-update) | async-done | bytes 8388624 | tf_op jit(solution)/shard_map/all_gather | solution.py:21
  605.7 39.1 %convolution_bitcast_fusion.1 = f32[4096,128]{0,1:T(8,128)} fusion(f32[4096,2048]{1,0:T(8,128)} %param.17, f32[16384,128]{0,1:T(8,128)} %all-gather.5.cloned.1.call-done, s32[]{:T(128)S(6)} %select_n.23), kind=kOutput, calls=%fused_computation.6 | convolution fusion | flops 12884901888 | bytes 36700164 | tf_op jit(solution)/shard_map/dot_general | solution.py:11
  644.9 65.2 %all-reduce.21.cloned.1.call-done = f32[4096,128]{0,1:T(8,128)} async-done(((f32[4096,128]{0,1:T(8,128)}), f32[4096,128]{0,1:T(8,128)}) %all-reduce.21.cloned.1.call-update) | async-done | bytes 2097168 | tf_op jit(solution)/shard_map/psum | solution.py:44
  710.1 6.3 fusion.5
  717.3 41.1 %all-reduce.23.cloned.1.call-done = f32[256,128]{1,0:T(8,128)} async-done(((f32[256,128]{1,0:T(8,128)}), f32[256,128]{1,0:T(8,128)}) %all-reduce.23.cloned.1.call-update) | async-done | bytes 131088 | tf_op jit(solution)/shard_map/psum | solution.py:45
  758.4 5.0 convolution_subtract_fusion.1
  763.4 4.1 fusion.4
  767.5 2.4 fusion.29
  770.8 42.0 %all-reduce.25.cloned.1.call-done = (f32[256,128]{1,0:T(8,128)}, f32[128,128]{0,1:T(8,128)}) async-done(((f32[256,128]{1,0:T(8,128)}, f32[128,128]{0,1:T(8,128)}), (f32[256,128]{1,0:T(8,128)}, f32[128,128]{0,1:T(8,128)})) %all-reduce.25.cloned.1.call-update) | async-done | bytes 196624 | tf_op jit(solution)/shard_map/psum | solution.py:47
  812.8 6.1 fusion
  818.9 2.0 fusion.8
  820.9 3.1 scatter.24
  824.5 11.7 %cholesky.81 = f32[128,128]{1,0:T(8,128)S(1)} custom-call(f32[128,128]{1,0:T(8,128)S(1)} %fusion.11), custom_call_target="Cholesky" | custom-call | tf_op jit(solution)/shard_map/jit(cholesky)/cholesky | solution.py:15
  836.9 0.7 fusion.17
  837.7 9.8 %custom-call.9 = f32[1,128,128]{1,2,0:T(8,128)S(1)} custom-call(f32[1,128,128]{2,1,0:T(8,128)S(1)} %get-tuple-element.89), custom_call_target="InvertDiagBlocksLowerTriangular" | custom-call | tf_op jit(solution)/shard_map/jit(_solve_triangular)/triangular_solve | solution.py:16
  847.5 3.6 convolution_bitcast_fusion
  851.2 3.1 maximum_multiply_fusion
  854.2 6.6 copy.18
  860.8 2.9 scatter.29
  863.7 0.7 copy-done.11
  864.4 0.7 copy-done.9
  (69 shorter events, 6.8 us)
Async XLA Ops:
  7.2 114.4 %all-reduce.13.cloned.1.call-start = ((), (), s32[]{:S(2)}) async-start(), calls=%async_computation | async-start | bytes 4194304 | tf_op jit(solution)/shard_map/psum | solution.py:33
  53.5 114.5 %all-reduce.15.cloned.1.call-start = ((), (), s32[]{:S(2)}) async-start(), calls=%async_computation.1 | async-start | bytes 131072 | tf_op jit(solution)/shard_map/psum | solution.py:34
  121.6 71.1 %copy-start.5 = (f32[4096,128]{0,1:T(8,128)S(1)}, f32[4096,128]{0,1:T(8,128)}, u32[]{:S(2)}) copy-start(f32[4096,128]{0,1:T(8,128)} %all-reduce.13.cloned.1.call-done) | copy-start | bytes 6291460
  126.4 157.2 %all-gather.3.cloned.1.call-start = ((), (), s32[]{:S(2)}) async-start(), calls=%async_computation.2 | async-start | bytes 10485760 | tf_op jit(solution)/shard_map/all_gather | solution.py:21
  196.0 192.1 %all-reduce.17.cloned.1.call-start = ((), (), s32[]{:S(2)}) async-start(), calls=%async_computation.3 | async-start | bytes 4194304 | tf_op jit(solution)/shard_map/psum | solution.py:44
  322.8 65.3 %copy-start = (f32[128,4096]{1,0:T(8,128)S(1)}, f32[128,4096]{1,0:T(8,128)}, u32[]{:S(2)}) copy-start(f32[128,4096]{1,0:T(8,128)} %fusion.2) | copy-start | bytes 6291460
  322.9 110.9 %all-reduce.19.cloned.1.call-start = ((), (), s32[]{:S(2)}) async-start(), calls=%async_computation.4 | async-start | bytes 131072 | tf_op jit(solution)/shard_map/psum | solution.py:45
  392.2 92.7 %all-reduce.27.cloned.1.call-start = ((), (), s32[]{:S(2)}) async-start(), calls=%async_computation.9 | async-start | bytes 262144 | tf_op jit(solution)/shard_map/psum | solution.py:47
  437.5 2.5 copy-start.3
  442.5 163.2 %all-gather.5.cloned.1.call-start = ((), (), s32[]{:S(2)}) async-start(), calls=%async_computation.5 | async-start | bytes 10485760 | tf_op jit(solution)/shard_map/all_gather | solution.py:21
  484.9 5.0 copy-start.8
  484.9 5.0 copy-start.13
  518.0 192.1 %all-reduce.21.cloned.1.call-start = ((), (), s32[]{:S(2)}) async-start(), calls=%async_computation.6 | async-start | bytes 4194304 | tf_op jit(solution)/shard_map/psum | solution.py:44
  644.8 113.6 %all-reduce.23.cloned.1.call-start = ((), (), s32[]{:S(2)}) async-start(), calls=%async_computation.7 | async-start | bytes 262144 | tf_op jit(solution)/shard_map/psum | solution.py:45
  716.4 96.3 %all-reduce.25.cloned.1.call-start = ((), (), s32[]{:S(2)}) async-start(), calls=%async_computation.8 | async-start | bytes 393216 | tf_op jit(solution)/shard_map/psum | solution.py:47
  758.4 5.0 copy-start.1
  763.4 4.1 copy-start.4
  767.5 3.1 copy-start.7
  812.8 6.1 copy-start.6
  812.8 6.1 copy-start.10
  812.8 11.2 %copy-start.12 = (f32[128,128]{0,1:T(8,128)S(1)}, f32[128,128]{0,1:T(8,128)}, u32[]{:S(2)}) copy-start(f32[128,128]{0,1:T(8,128)} %get-tuple-element.81) | copy-start | bytes 196612
  847.5 3.7 copy-start.2
  863.6 0.7 copy-start.11
  864.4 0.7 copy-start.9
Sparse Core Ops, SparseCore 0:
  53.6 67.8 all-reduce.12
  126.5 41.4 all-reduce.14
  196.1 87.4 all-gather.2
  323.0 65.0 all-reduce.16
  392.3 41.4 all-reduce.18
  442.6 42.2 all-reduce.26
  518.1 87.4 all-gather.4
  645.0 65.1 all-reduce.20
  716.5 41.8 all-reduce.22
  770.1 42.6 all-reduce.24
where the time goes:
time: 877 us; the launch traced here: 872 us
  waiting for transfers between devices  581 us (66%)
  matrix products  137 us (16%)
  other arithmetic  77.5 us (9%)
  local copies, waits for them, and re-layouts  59.9 us (7%)
  between operations  14.7 us (2%)
    all_gather x2, waiting for transfers between devices, transpose_block(): whole = lax.all_gather(current, 'row', axis=0, tiled=True)  174 us
    psum x2, waiting for transfers between devices, local(): image = lax.psum(partial_value, 'col')  130 us
    dot_general x15, matrix products, product(): jnp.dot(left, right, precision=lax.Precision.HIGHEST, preferred_element_t...  125 us
    psum x2, waiting for transfers between devices, local(): lax.psum((product(stacked.T, once), product(once.T, once)), 'row')  84.2 us
    psum x2, waiting for transfers between devices, local(): first = lax.psum(product(stacked.T, image), 'row')  82.5 us
    psum x1, waiting for transfers between devices, local(): start = lax.psum(jnp.where(inside[None, :], picked, 0.0), 'col')  68 us
    psum x1, waiting for transfers between devices, local(): gram = lax.psum(product(start.T, start), 'row')  41.3 us
    unnamed x30, local copies, waits for them, and re-layouts  39.2 us
  transfers between devices with their start and end apart: 10, of which 10 were waited for; matrix products, arithmetic and copies ran while one was open for 0% of the time, Pallas kernels for 0%

commit v1 on v0

--- a/solution.py
+++ b/solution.py
@@ -1,3 +1,4 @@
+import functools
 import jax
 import jax.numpy as jnp
 from jax import lax
@@ -5,6 +6,21 @@
 
 N = 16384
 ITERS = 2
+
+
+def store_the_table(sheet, axis_name):
+    slots = jax.lax.axis_size(axis_name)
+    d_next = sheet
+    for ii in [it for it in (1, 2, 4, 8, 16) if it < slots]:
+        f_next = range(slots)
+        w_next = map(lambda dev_j: (dev_j, dev_j ^ ii), f_next)
+        part_next = list(w_next)
+        r_now = jax.lax.ppermute(d_next, axis_name, part_next)
+        d_next = d_next + r_now
+    return d_next
+
+
+lift_side = functools.partial(store_the_table, axis_name="col")
 
 
 def product(left, right):
@@ -41,7 +57,7 @@
         vector = transpose_block(full, col_place, col_count)
         partial_value = product(covariance, vector)
         stacked = jnp.concatenate(blocks, axis=1)
-        image = lax.psum(partial_value, "col")
+        image = lift_side(partial_value)
         first = lax.psum(product(stacked.T, image), "row")
         once = image - product(stacked, first)
         second, raw_gram = lax.psum((product(stacked.T, once), product(once.T, once)), "row")

time: 877 us -> 1040 us (1.19)
  waiting for transfers between devices: 581 us -> 731 us
    ppermute x0 -> x6, waiting for transfers between devices: none -> 280 us  [store_the_table(): r_now = jax.lax.ppermute(d_next, axis_name, part_next)]
    psum x2 -> x0, waiting for transfers between devices: 130 us -> none  [local(): image = lax.psum(partial_value, 'col')]
    unnamed x30 -> x38, local copies, waits for them, and re-layouts: 39.2 us -> 43.1 us
  transfers between devices with their start and end apart: 10 -> 14, of which waited for: 10 -> 14; matrix products, arithmetic and copies ran while one was open for 0% -> 0% of each run, Pallas kernels for 0% -> 0%
where the time goes in v1:
time: 1040 us; the launch traced here: 1030 us
  waiting for transfers between devices  731 us (70%)
  matrix products  133 us (13%)
  other arithmetic  82.3 us (8%)
  local copies, waits for them, and re-layouts  63.8 us (6%)
  between operations  14.8 us (1%)
    ppermute x6, waiting for transfers between devices, store_the_table(): r_now = jax.lax.ppermute(d_next, axis_name, part_next)  280 us
    all_gather x2, waiting for transfers between devices, transpose_block(): whole = lax.all_gather(current, 'row', axis=0, tiled=True)  174 us
    dot_general x15, matrix products, product(): jnp.dot(left, right, precision=lax.Precision.HIGHEST, preferred_element_t...  121 us
    psum x2, waiting for transfers between devices, local(): lax.psum((product(stacked.T, once), product(once.T, once)), 'row')  84.2 us
    psum x2, waiting for transfers between devices, local(): first = lax.psum(product(stacked.T, image), 'row')  83.2 us
    psum x1, waiting for transfers between devices, local(): start = lax.psum(jnp.where(inside[None, :], picked, 0.0), 'col')  68 us
    unnamed x38, local copies, waits for them, and re-layouts  43.1 us
    psum x1, waiting for transfers between devices, local(): gram = lax.psum(product(start.T, start), 'row')  41.3 us
  transfers between devices with their start and end apart: 14, of which 14 were waited for; matrix products, arithmetic and copies ran while one was open for 0% of the time, Pallas kernels for 0%

profile of v1, /device:TPU:0, one launch (start us, length us, event | category | flops | bytes accessed | tf_op | source)
XLA Modules:
  0.0 1034.8 jit_solution(2351387053976268932)
XLA Ops:
  7.9 31.1 %copy.5 = f32[4096,2048]{0,1:T(8,128)} copy(f32[4096,2048]{1,0:T(8,128)} %param.17) | data formatting | bytes 67108864 | tf_op args[0]
  39.0 12.8 %gather_fusion = f32[128,4096]{1,0:T(8,128)S(1)} fusion(f32[4096,2048]{0,1:T(8,128)} %copy.5, s32[1024]{0:T(1024)S(1)} %pad_clamp_fusion), kind=kCustom, calls=%fused_computation | custom fusion | bytes 4194816 | tf_op jit(solution)/shard_map/jit(_take)/gather | solution.py:48
  51.8 1.7 select_bitcast_fusion
  53.5 68.0 %all-reduce.11.cloned.1.call-done = f32[4096,128]{0,1:T(8,128)} async-done(((f32[4096,128]{0,1:T(8,128)}), f32[4096,128]{0,1:T(8,128)}) %all-reduce.11.cloned.1.call-update) | async-done | bytes 2097168 | tf_op jit(solution)/shard_map/psum | solution.py:49
  121.5 4.8 fusion.27
  126.7 41.3 %all-reduce.13.cloned.1.call-done = f32[128,128]{0,1:T(8,128)} async-done(((f32[128,128]{0,1:T(8,128)}), f32[128,128]{0,1:T(8,128)}) %all-reduce.13.cloned.1.call-update) | async-done | bytes 65552 | tf_op jit(solution)/shard_map/psum | solution.py:50
  169.8 11.7 %cholesky.59 = f32[128,128]{1,0:T(8,128)S(1)} custom-call(f32[128,128]{1,0:T(8,128)S(1)} %fusion.15), custom_call_target="Cholesky" | custom-call | tf_op jit(solution)/shard_map/jit(cholesky)/cholesky | solution.py:31
  182.8 9.8 custom-call.7
  192.7 3.2 fusion.2
  196.5 87.1 %all-gather.3.cloned.1.call-done = f32[16384,128]{0,1:T(8,128)} async-done(((f32[4096,128]{0,1:T(8,128)}), f32[16384,128]{0,1:T(8,128)}) %all-gather.3.cloned.1.call-update) | async-done | bytes 8388624 | tf_op jit(solution)/shard_map/all_gather | solution.py:37
  283.6 38.4 %convolution_bitcast_fusion.3 = f32[4096,128]{0,1:T(8,128)S(1)} fusion(f32[4096,2048]{1,0:T(8,128)} %param.17, f32[16384,128]{0,1:T(8,128)} %all-gather.3.cloned.1.call-done, s32[]{:T(128)S(6)} %select_n.23), kind=kOutput, calls=%fused_computation.11 | convolution fusion | flops 12884901888 | bytes 36700164 | tf_op jit(solution)/shard_map/dot_general | solution.py:27
  323.3 2.9 collective-permute-done
  326.2 1.9 add.77
  329.6 46.2 %collective-permute-done.1 = f32[4096,128]{0,1:T(8,128)S(1)} collective-permute-done((f32[4096,128]{0,1:T(8,128)S(1)}, f32[4096,128]{0,1:T(8,128)S(1)}, u32[]{:S(2)}, u32[]{:S(2)}) %collective-permute-start.1) | collective-permute-done | bytes 2097184 | tf_op jit(solution)/shard_map/ppermute | solution.py:18
  376.1 2.5 collective-permute-start.2
  378.5 90.3 %collective-permute-done.2 = f32[4096,128]{0,1:T(8,128)S(1)} collective-permute-done((f32[4096,128]{0,1:T(8,128)S(1)}, f32[4096,128]{0,1:T(8,128)S(1)}, u32[]{:S(2)}, u32[]{:S(2)}) %collective-permute-start.2) | collective-permute-done | bytes 2097184 | tf_op jit(solution)/shard_map/ppermute | solution.py:18
  470.4 2.5 fusion.28
  473.1 41.7 %all-reduce.15.cloned.1.call-done = f32[128,128]{1,0:T(8,128)} async-done(((f32[128,128]{1,0:T(8,128)}), f32[128,128]{1,0:T(8,128)}) %all-reduce.15.cloned.1.call-update) | async-done | bytes 65552 | tf_op jit(solution)/shard_map/psum | solution.py:61
  514.9 3.7 convolution_subtract_fusion.3
  518.6 2.4 fusion.29
  521.0 2.5 fusion.30
  523.8 42.2 %all-reduce.21.cloned.1.call-done = (f32[128,128]{1,0:T(8,128)}, f32[128,128]{0,1:T(8,128)}) async-done(((f32[128,128]{1,0:T(8,128)}, f32[128,128]{0,1:T(8,128)}), (f32[128,128]{1,0:T(8,128)}, f32[128,128]{0,1:T(8,128)})) %all-reduce.21.cloned.1.call-update) | async-done | bytes 131088 | tf_op jit(solution)/shard_map/psum | solution.py:63
  566.0 5.0 fusion.1
  571.3 11.7 %cholesky.70 = f32[128,128]{1,0:T(8,128)S(1)} custom-call(f32[128,128]{1,0:T(8,128)S(1)} %fusion.13), custom_call_target="Cholesky" | custom-call | tf_op jit(solution)/shard_map/jit(cholesky)/cholesky | solution.py:31
  584.4 9.8 custom-call.8
  594.2 4.9 convolution_bitcast_fusion.2
  599.6 87.2 %all-gather.5.cloned.1.call-done = f32[16384,128]{0,1:T(8,128)} async-done(((f32[4096,128]{0,1:T(8,128)}), f32[16384,128]{0,1:T(8,128)}) %all-gather.5.cloned.1.call-update) | async-done | bytes 8388624 | tf_op jit(solution)/shard_map/all_gather | solution.py:37
  686.8 39.1 %convolution_bitcast_fusion.1 = f32[4096,128]{0,1:T(8,128)} fusion(f32[4096,2048]{1,0:T(8,128)} %param.17, f32[16384,128]{0,1:T(8,128)} %all-gather.5.cloned.1.call-done, s32[]{:T(128)S(6)} %select_n.23), kind=kOutput, calls=%fused_computation.6 | convolution fusion | flops 12884901888 | bytes 36700164 | tf_op jit(solution)/shard_map/dot_general | solution.py:27
  725.9 4.4 collective-permute-done.3
  730.3 1.9 add.80
  733.7 46.2 %collective-permute-done.4 = f32[4096,128]{0,1:T(8,128)S(1)} collective-permute-done((f32[4096,128]{0,1:T(8,128)S(1)}, f32[4096,128]{0,1:T(8,128)S(1)}, u32[]{:S(2)}, u32[]{:S(2)}) %collective-permute-start.4) | collective-permute-done | bytes 2097184 | tf_op jit(solution)/shard_map/ppermute | solution.py:18
  780.1 2.5 collective-permute-start.5
  782.6 90.2 %collective-permute-done.5 = f32[4096,128]{0,1:T(8,128)S(1)} collective-permute-done((f32[4096,128]{0,1:T(8,128)S(1)}, f32[4096,128]{0,1:T(8,128)S(1)}, u32[]{:S(2)}, u32[]{:S(2)}) %collective-permute-start.5) | collective-permute-done | bytes 2097184 | tf_op jit(solution)/shard_map/ppermute | solution.py:18
  874.5 4.1 fusion.5
  879.5 41.5 %all-reduce.17.cloned.1.call-done = f32[256,128]{1,0:T(8,128)} async-done(((f32[256,128]{1,0:T(8,128)}), f32[256,128]{1,0:T(8,128)}) %all-reduce.17.cloned.1.call-update) | async-done | bytes 131088 | tf_op jit(solution)/shard_map/psum | solution.py:61
  921.0 5.0 convolution_subtract_fusion.1
  926.0 4.1 fusion.4
  930.1 2.4 fusion.31
  933.3 42.0 %all-reduce.19.cloned.1.call-done = (f32[256,128]{1,0:T(8,128)}, f32[128,128]{0,1:T(8,128)}) async-done(((f32[256,128]{1,0:T(8,128)}, f32[128,128]{0,1:T(8,128)}), (f32[256,128]{1,0:T(8,128)}, f32[128,128]{0,1:T(8,128)})) %all-reduce.19.cloned.1.call-update) | async-done | bytes 196624 | tf_op jit(solution)/shard_map/psum | solution.py:63
  975.3 6.1 fusion
  981.5 2.0 fusion.8
  983.5 3.1 scatter.24
  987.1 11.7 %cholesky.81 = f32[128,128]{1,0:T(8,128)S(1)} custom-call(f32[128,128]{1,0:T(8,128)S(1)} %fusion.11), custom_call_target="Cholesky" | custom-call | tf_op jit(solution)/shard_map/jit(cholesky)/cholesky | solution.py:31
  1000.2 9.8 custom-call.9
  1010.1 3.6 convolution_bitcast_fusion
  1013.7 3.1 maximum_multiply_fusion
  1016.8 6.6 copy.18
  1023.3 2.9 scatter.29
  (89 shorter events, 20.8 us)
Async XLA Ops:
  7.2 114.4 %all-reduce.11.cloned.1.call-start = ((), (), s32[]{:S(2)}) async-start(), calls=%async_computation | async-start | bytes 4194304 | tf_op jit(solution)/shard_map/psum | solution.py:49
  53.5 114.5 %all-reduce.13.cloned.1.call-start = ((), (), s32[]{:S(2)}) async-start(), calls=%async_computation.1 | async-start | bytes 131072 | tf_op jit(solution)/shard_map/psum | solution.py:50
  121.5 71.1 %copy-start.8 = (f32[4096,128]{0,1:T(8,128)S(1)}, f32[4096,128]{0,1:T(8,128)}, u32[]{:S(2)}) copy-start(f32[4096,128]{0,1:T(8,128)} %all-reduce.11.cloned.1.call-done) | copy-start | bytes 6291460
  126.4 157.2 %all-gather.3.cloned.1.call-start = ((), (), s32[]{:S(2)}) async-start(), calls=%async_computation.2 | async-start | bytes 10485760 | tf_op jit(solution)/shard_map/all_gather | solution.py:37
  195.9 318.9 %all-reduce.15.cloned.1.call-start = ((), (), s32[]{:S(2)}) async-start(), calls=%async_computation.3 | async-start | bytes 131072 | tf_op jit(solution)/shard_map/psum | solution.py:61
  321.9 1.3 copy-start.9
  322.0 4.2 collective-permute-start
  328.0 47.7 %collective-permute-start.1 = (f32[4096,128]{0,1:T(8,128)S(1)}, f32[4096,128]{0,1:T(8,128)S(1)}, u32[]{:S(2)}, u32[]{:S(2)}) collective-permute-start(f32[4096,128]{0,1:T(8,128)S(1)} %add.77), channel_id=1, source_target_pairs={{0,2},{1,3},{2,0},{3,1},{4,6},{5,7},{6,4},{7,5},{8,10},{9,11},{10,... | collective-permute-start | bytes 6291464 | tf_op jit(solution)/shard_map/ppermute | solution.py:18
  376.1 94.3 %copy-start = (f32[128,4096]{1,0:T(8,128)S(1)}, f32[128,4096]{1,0:T(8,128)}, u32[]{:S(2)}) copy-start(f32[128,4096]{1,0:T(8,128)} %fusion.2) | copy-start | bytes 6291460
  376.1 92.7 %collective-permute-start.2 = (f32[4096,128]{0,1:T(8,128)S(1)}, f32[4096,128]{0,1:T(8,128)S(1)}, u32[]{:S(2)}, u32[]{:S(2)}) collective-permute-start(f32[4096,128]{0,1:T(8,128)S(1)} %add.78), channel_id=1, source_target_pairs={{0,4},{1,5},{2,6},{3,7},{4,0},{5,1},{6,2},{7,3},{8,12},{9,13},{10,... | collective-permute-start | bytes 6291464 | tf_op jit(solution)/shard_map/ppermute | solution.py:18
  469.1 1.3 copy-start.6
  472.9 93.0 %all-reduce.21.cloned.1.call-start = ((), (), s32[]{:S(2)}) async-start(), calls=%async_computation.7 | async-start | bytes 262144 | tf_op jit(solution)/shard_map/psum | solution.py:63
  518.6 2.5 copy-start.4
  523.5 163.2 %all-gather.5.cloned.1.call-start = ((), (), s32[]{:S(2)}) async-start(), calls=%async_computation.4 | async-start | bytes 10485760 | tf_op jit(solution)/shard_map/all_gather | solution.py:37
  565.9 5.0 copy-start.12
  566.0 5.0 copy-start.17
  599.1 321.8 %all-reduce.17.cloned.1.call-start = ((), (), s32[]{:S(2)}) async-start(), calls=%async_computation.5 | async-start | bytes 262144 | tf_op jit(solution)/shard_map/psum | solution.py:61
  725.9 4.4 collective-permute-start.3
  732.1 47.7 %collective-permute-start.4 = (f32[4096,128]{0,1:T(8,128)S(1)}, f32[4096,128]{0,1:T(8,128)S(1)}, u32[]{:S(2)}, u32[]{:S(2)}) collective-permute-start(f32[4096,128]{0,1:T(8,128)S(1)} %add.80), channel_id=1, source_target_pairs={{0,2},{1,3},{2,0},{3,1},{4,6},{5,7},{6,4},{7,5},{8,10},{9,11},{10,... | collective-permute-start | bytes 6291464 | tf_op jit(solution)/shard_map/ppermute | solution.py:18
  780.1 94.4 %copy-start.1 = (f32[4096,128]{0,1:T(8,128)S(1)}, f32[4096,128]{0,1:T(8,128)}, u32[]{:S(2)}) copy-start(f32[4096,128]{0,1:T(8,128)} %convolution_bitcast_fusion.2) | copy-start | bytes 6291460
  780.1 92.7 %collective-permute-start.5 = (f32[4096,128]{0,1:T(8,128)S(1)}, f32[4096,128]{0,1:T(8,128)S(1)}, u32[]{:S(2)}, u32[]{:S(2)}) collective-permute-start(f32[4096,128]{0,1:T(8,128)S(1)} %add.81), channel_id=1, source_target_pairs={{0,4},{1,5},{2,6},{3,7},{4,0},{5,1},{6,2},{7,3},{8,12},{9,13},{10,... | collective-permute-start | bytes 6291464 | tf_op jit(solution)/shard_map/ppermute | solution.py:18
  873.2 1.3 copy-start.7
  878.6 96.7 %all-reduce.19.cloned.1.call-start = ((), (), s32[]{:S(2)}) async-start(), calls=%async_computation.6 | async-start | bytes 393216 | tf_op jit(solution)/shard_map/psum | solution.py:63
  921.0 5.0 copy-start.2
  926.0 4.1 copy-start.5
  930.1 3.1 copy-start.11
  975.3 6.1 copy-start.10
  975.3 6.1 copy-start.14
  975.3 11.2 %copy-start.16 = (f32[128,128]{0,1:T(8,128)S(1)}, f32[128,128]{0,1:T(8,128)}, u32[]{:S(2)}) copy-start(f32[128,128]{0,1:T(8,128)} %get-tuple-element.81) | copy-start | bytes 196612
  1010.1 3.7 copy-start.3
  1026.2 0.7 copy-start.15
  1027.0 0.7 copy-start.13
Sparse Core Ops, SparseCore 0:
  53.6 67.8 all-reduce.10
  126.5 41.4 all-reduce.12
  196.0 87.4 all-gather.2
  473.0 41.7 all-reduce.14
  523.6 42.2 all-reduce.20
  599.2 87.4 all-gather.4
  878.7 42.1 all-reduce.16
  932.6 42.6 all-reduce.18
